TPU v7x, 32 devices: a whole 2x2x4 slice. The times are simulated.
32 devices in a mesh: dom: 8 (over y, x, core), dim: 4 (over z).
Axes of the slice: x: 2, y: 2, z: 4, core: 2. Of those that a mesh axis runs over, the one named last changes fastest.
Arguments:
- particles: float32 [64, 1024], P('dom', 'dim'), may hold values from -5 to 5
- data_rows: bfloat16 [64, 16, 1024], P('dom', None, 'dim'), may hold values from -0.375 to 0.375
- labels: int32 [64, 16], P('dom'), may hold values from 0 to 1
Outputs:
- updates: float32 [2, 64, 1024], P(None, 'dom', 'dim')
All inputs are finite; a program needn't handle non-finite values.
Results may differ from a plain program's by a relative error of at most 0.0003.
Values may be sent and summed in bfloat16 or wider, within the bound.
A program may use at most 64 MiB of HBM per device.

v0:
```python
from functools import partial
import jax
import jax.numpy as jnp
from jax import lax
from jax.sharding import PartitionSpec as P

NEWTON = 2
CG_STEPS = 2
BAND = 1
prior_precision = 0.05
like_weight = 4.0
move_size = 0.5
highest = lax.Precision.HIGHEST


def drift_terms(x_local, squares, kernel_scale, rows_pos, rows_grad):
    inner_rows = jnp.einsum("id,jd->ij", x_local, rows_pos, precision=highest)
    row_squares = jnp.sum(rows_pos * rows_pos, axis=1)
    distance = squares[:, None] + row_squares[None, :] - 2.0 * inner_rows
    kernel = jnp.exp(-distance / kernel_scale)
    kernel_sq = kernel * kernel
    kernel_grad = jnp.dot(kernel, rows_grad, precision=highest)
    kernel_pos = jnp.dot(kernel, rows_pos, precision=highest)
    square_pos = jnp.dot(kernel_sq, rows_pos, precision=highest)
    return (
        kernel,
        kernel_grad,
        kernel_pos,
        square_pos,
        jnp.sum(kernel, axis=1),
        jnp.sum(kernel_sq, axis=1),
    )


def pair_block(running, piece, start, kernel, curve_rows, pos_rows, vectors, cross_scale):
    weight_sq = (kernel * kernel).T
    factor_part = piece.astype(jnp.float32)
    projected = jnp.einsum("jrd,id->jri", factor_part, vectors, precision=highest)
    weighted = projected * curve_rows[:, :, None] * weight_sq[:, None, :]
    running = jnp.einsum("jrd,jri->id", factor_part, weighted, precision=highest)
    along_pair = jnp.einsum("jd,id->ji", pos_rows, vectors, precision=highest)
    return running + cross_scale * jnp.einsum(
        "ji,jd->id", weight_sq * along_pair, pos_rows, precision=highest
    )


def residual_sum(vectors):
    return lax.psum(jnp.sum(vectors * vectors), ("dom", "dim"))


def per_device(particles, data_rows, labels):
    dim_count = lax.axis_size("dim")
    dom_count = lax.axis_size("dom")
    part_rows = particles.shape[0]
    slice_width = particles.shape[1]
    width = slice_width * dim_count
    quarter = part_rows // dim_count
    total_count = part_rows * dom_count
    kernel_scale = 1.0 * BAND * width
    cross_scale = 4.0 / (kernel_scale * kernel_scale)
    lane = lax.axis_index("dim")
    first_row = lane * quarter
    first_col = lane * slice_width
    own_factors = lax.all_to_all(data_rows, "dim", split_axis=0, concat_axis=2, tiled=True)
    factor_float = own_factors.astype(jnp.float32)
    own_targets = lax.dynamic_slice_in_dim(labels, first_row, quarter, 0).astype(jnp.float32)
    current = particles
    outputs = []
    for newton_step in range(NEWTON):
        x_local = lax.all_gather(current, "dim", axis=1, tiled=True)
        own_pos = lax.dynamic_slice_in_dim(x_local, first_row, quarter, 0)
        logits = jnp.einsum("jrd,jd->jr", factor_float, own_pos, precision=highest)
        probs = jax.nn.sigmoid(logits)
        own_grad = -prior_precision * own_pos + like_weight * jnp.einsum(
            "jr,jrd->jd", own_targets - probs, factor_float, precision=highest
        )
        own_curve = like_weight * probs * (1.0 - probs)
        pos_rows, grad_rows, curve_rows = (
            lax.all_gather(own_pos, "dom", axis=0, tiled=True),
            lax.all_gather(own_grad, "dom", axis=0, tiled=True),
            lax.all_gather(own_curve, "dom", axis=0, tiled=True),
        )
        squares = jnp.sum(x_local * x_local, axis=1)
        kernel, kernel_grad, kernel_pos, square_pos, kernel_total, square_total = drift_terms(
            x_local, squares, kernel_scale, pos_rows, grad_rows
        )
        kernel_grad, kernel_pos, square_pos, kernel_total, square_total = lax.psum(
            (kernel_grad, kernel_pos, square_pos, kernel_total, square_total), "dim"
        )
        drift_full = (
            kernel_grad + 2.0 / kernel_scale * (x_local * kernel_total[:, None] - kernel_pos)
        ) / total_count
        drift = lax.dynamic_slice_in_dim(drift_full, first_col, slice_width, 1)
        mean_slice = lax.dynamic_slice_in_dim(square_pos, first_col, slice_width, 1)
        solution = jnp.zeros_like(drift)
        residual = drift
        direction = drift
        norm_now = residual_sum(residual)
        for solve_step in range(CG_STEPS):
            vectors_full = lax.all_gather(direction, "dim", axis=1, tiled=True)
            start_total = jnp.zeros((part_rows, width), jnp.float32)
            block_step = partial(
                pair_block,
                kernel=kernel,
                curve_rows=curve_rows,
                pos_rows=pos_rows,
                vectors=vectors_full,
                cross_scale=cross_scale,
            )
            pairs = block_step(
                start_total, lax.all_gather(own_factors, "dom", axis=0, tiled=True), jnp.int32(0)
            )
            pairs = lax.psum_scatter(pairs, "dim", scatter_dimension=1, tiled=True)
            along_self = jnp.sum(x_local * vectors_full, axis=1)
            along_mean = jnp.sum(vectors_full * square_pos, axis=1)
            local = prior_precision * square_total[:, None] * direction + cross_scale * (
                current * (along_self * square_total - along_mean)[:, None]
                - along_self[:, None] * mean_slice
            )
            image = (pairs + local) / total_count
            curve_total, mixed_total, image_square = lax.psum(
                (jnp.sum(direction * image), jnp.sum(residual * image), jnp.sum(image * image)),
                ("dom", "dim"),
            )
            alpha = norm_now / curve_total
            norm_next = norm_now - 2.0 * alpha * mixed_total + alpha * alpha * image_square
            solution = solution + alpha * direction
            residual = residual - alpha * image
            if solve_step + 1 < CG_STEPS:
                direction = residual + norm_next / norm_now * direction
                norm_now = norm_next
        outputs.append(solution)
        current = current + move_size * solution
    return jnp.stack(outputs)


def solution(mesh):
    placed = (P("dom", "dim"), P("dom", None, "dim"), P("dom", None))
    return jax.shard_map(
        per_device, mesh=mesh, in_specs=placed, out_specs=P(None, "dom", "dim"), check_vma=False
    )
```

profile of v0, /device:TPU:12, one launch (start us, length us, event | category | flops | bytes accessed | tf_op | source)
XLA Modules:
  0.0 489.8 jit_solution(9462814069500571010)
XLA Ops:
  6.5 5.3 %all-to-all-start = ((bf16[8,16,256]{2,1,0:T(8,128)(2,1)}), bf16[8,16,256]{2,1,0:T(8,128)(2,1)S(1)}, u32[]{:S(2)}, u32[]{:S(2)}) async-start(bf16[8,16,256]{2,1,0:T(8,128)(2,1)} %param.4), calls=%async_computation | async-start | bytes 131072 | tf_op jit(solution)/shard_map/all_to_all | solution.py:64
  12.6 13.1 %all_gather.42 = f32[8,1024]{1,0:T(8,128)S(1)} all-gather(f32[8,256]{1,0:T(8,128)S(1)} %copy-done.2), channel_id=1, replica_groups=mesh['dom'=8,'dim'=4] {'dim'}, dimensions={1}, use_global_device_ids=true | all-gather | bytes 40960 | tf_op jit(solution)/shard_map/all_gather | solution.py:70
  27.0 9.2 %all-gather = f32[8,2,1024]{2,1,0:T(2,128)S(1)} all-gather(f32[1,2,1024]{2,1,0:T(2,128)S(1)} %get-tuple-element.47), channel_id=1, replica_groups=mesh['dom'=8,'dim'=4] {'dom'}, dimensions={0}, use_global_device_ids=true | all-gather | bytes 73728 | tf_op jit(solution)/shard_map/all_gather | solution.py:79
  39.0 8.3 %all-gather.1 = f32[8,2,1024]{2,1,0:T(2,128)S(1)} all-gather(f32[1,2,1024]{2,1,0:T(2,128)S(1)} %get-tuple-element.48), channel_id=1, replica_groups=mesh['dom'=8,'dim'=4] {'dom'}, dimensions={0}, use_global_device_ids=true | all-gather | bytes 73728 | tf_op jit(solution)/shard_map/all_gather | solution.py:80
  48.2 8.9 %all-gather.2 = f32[8,2,16]{2,1,0:T(2,128)S(1)} all-gather(f32[1,2,16]{2,1,0:T(2,128)S(1)} %get-tuple-element.43), channel_id=1, replica_groups=mesh['dom'=8,'dim'=4] {'dom'}, dimensions={0}, use_global_device_ids=true | all-gather | bytes 1152 | tf_op jit(solution)/shard_map/all_gather | solution.py:81
  57.2 8.9 %all_gather.46 = bf16[16,16,1024]{2,1,0:T(8,128)(2,1)S(1)} all-gather(bf16[2,16,1024]{2,1,0:T(8,128)(2,1)S(1)} %all_to_all.16), channel_id=1, replica_groups=mesh['dom'=8,'dim'=4] {'dom'}, dimensions={0}, use_global_device_ids=true | all-gather | bytes 589824 | tf_op jit(solution)/shard_map/all_gather | solution.py:111
  66.1 26.1 %all-reduce.9.cloned.1.call-done = (f32[8,1024]{1,0:T(8,128)}, f32[8,1024]{1,0:T(8,128)}, f32[8]{0:T(128)}, f32[8,1024]{1,0:T(8,128)}, f32[8]{0:T(128)}) async-done(((f32[8,1024]{1,0:T(8,128)}, f32[8,1024]{1,0:T(8,128)}, f32[8]{0:T(128)}, f32[8,1024]{1,0:T(8,128)}, f32[8]{0:T(128)}), (f32[8,1024]{1,0:T(8,128)}, f32[8,1024]{1,0:T(8,128)}, f32[8]{0:T(128)}, f32[8,1024]{1,0:T(8,128)}, ...) | async-done | bytes 98384 | tf_op jit(solution)/shard_map/psum | solution.py:87
  93.6 12.2 %all_gather.45 = f32[8,1024]{1,0:T(8,128)S(1)} all-gather(f32[8,256]{1,0:T(8,128)S(1)} %fusion.18), channel_id=1, replica_groups=mesh['dom'=8,'dim'=4] {'dim'}, dimensions={1}, use_global_device_ids=true | all-gather | bytes 40960 | tf_op jit(solution)/shard_map/all_gather | solution.py:100
  106.7 1.9 fusion.4
  110.8 16.8 %reduce-scatter.5.cloned.1.call-done = f32[8,256]{1,0:T(8,128)} async-done(((f32[8,1024]{1,0:T(8,128)}), f32[8,256]{1,0:T(8,128)}) %reduce-scatter.5.cloned.1.call-update) | async-done | bytes 8208 | tf_op jit(solution)/shard_map/reduce_scatter | solution.py:113
  127.6 1.5 multiply_reduce_fusion.17
  129.1 43.2 %all-reduce.1 = (f32[]{:T(128)}, f32[]{:T(128)}, f32[]{:T(128)}) all-reduce(f32[]{:T(128)} %get-tuple-element.18, f32[]{:T(128)} %get-tuple-element.17, f32[]{:T(128)} %get-tuple-element.16), channel_id=1, replica_groups=mesh['dom'=8,'dim'=4] {'dom','dim'}, use_global_device_ids=true, to_apply=%region_7.0 | all-reduce | flops 3 | bytes 24 | tf_op jit(solution)/shard_map/psum | solution.py:48
  176.2 11.4 %all_gather.48 = f32[8,1024]{1,0:T(8,128)S(1)} all-gather(f32[8,256]{1,0:T(8,128)S(1)} %multiply_add_fusion.3), channel_id=1, replica_groups=mesh['dom'=8,'dim'=4] {'dim'}, dimensions={1}, use_global_device_ids=true | all-gather | bytes 40960 | tf_op jit(solution)/shard_map/all_gather | solution.py:100
  187.9 2.0 fusion.5
  191.4 16.5 %reduce-scatter.7.cloned.1.call-done = f32[8,256]{1,0:T(8,128)} async-done(((f32[8,1024]{1,0:T(8,128)}), f32[8,256]{1,0:T(8,128)}) %reduce-scatter.7.cloned.1.call-update) | async-done | bytes 8208 | tf_op jit(solution)/shard_map/reduce_scatter | solution.py:113
  208.0 1.4 multiply_reduce_fusion.16
  209.4 43.1 %psum.140 = f32[]{:T(128)} all-reduce(f32[]{:T(128)} %multiply_reduce_fusion.16), channel_id=1, replica_groups=mesh['dom'=8,'dim'=4] {'dom','dim'}, use_global_device_ids=true, to_apply=%region_22.0 | all-reduce | flops 1 | bytes 8 | tf_op jit(solution)/shard_map/psum | solution.py:121
  253.2 11.3 %all_gather.49 = f32[8,1024]{1,0:T(8,128)S(1)} all-gather(f32[8,256]{1,0:T(8,128)S(1)} %get-tuple-element.50), channel_id=1, replica_groups=mesh['dom'=8,'dim'=4] {'dim'}, dimensions={1}, use_global_device_ids=true | all-gather | bytes 40960 | tf_op jit(solution)/shard_map/all_gather | solution.py:70
  265.0 8.3 %all-gather.3 = f32[8,2,1024]{2,1,0:T(2,128)S(1)} all-gather(f32[1,2,1024]{2,1,0:T(2,128)S(1)} %get-tuple-element.45), channel_id=1, replica_groups=mesh['dom'=8,'dim'=4] {'dom'}, dimensions={0}, use_global_device_ids=true | all-gather | bytes 73728 | tf_op jit(solution)/shard_map/all_gather | solution.py:79
  276.0 9.2 %all-gather.4 = f32[8,2,1024]{2,1,0:T(2,128)S(1)} all-gather(f32[1,2,1024]{2,1,0:T(2,128)S(1)} %get-tuple-element.46), channel_id=1, replica_groups=mesh['dom'=8,'dim'=4] {'dom'}, dimensions={0}, use_global_device_ids=true | all-gather | bytes 73728 | tf_op jit(solution)/shard_map/all_gather | solution.py:80
  286.3 8.0 %all-gather.5 = f32[8,2,16]{2,1,0:T(2,128)S(1)} all-gather(f32[1,2,16]{2,1,0:T(2,128)S(1)} %get-tuple-element.40), channel_id=1, replica_groups=mesh['dom'=8,'dim'=4] {'dom'}, dimensions={0}, use_global_device_ids=true | all-gather | bytes 1152 | tf_op jit(solution)/shard_map/all_gather | solution.py:81
  294.3 26.9 %all-reduce.7.cloned.1.call-done = (f32[8,1024]{1,0:T(8,128)}, f32[8,1024]{1,0:T(8,128)}, f32[8]{0:T(128)}, f32[8,1024]{1,0:T(8,128)}, f32[8]{0:T(128)}) async-done(((f32[8,1024]{1,0:T(8,128)}, f32[8,1024]{1,0:T(8,128)}, f32[8]{0:T(128)}, f32[8,1024]{1,0:T(8,128)}, f32[8]{0:T(128)}), (f32[8,1024]{1,0:T(8,128)}, f32[8,1024]{1,0:T(8,128)}, f32[8]{0:T(128)}, f32[8,1024]{1,0:T(8,128)}, ...) | async-done | bytes 98384 | tf_op jit(solution)/shard_map/psum | solution.py:87
  322.6 12.4 %all_gather.52 = f32[8,1024]{1,0:T(8,128)S(1)} all-gather(f32[8,256]{1,0:T(8,128)S(1)} %fusion.16), channel_id=1, replica_groups=mesh['dom'=8,'dim'=4] {'dim'}, dimensions={1}, use_global_device_ids=true | all-gather | bytes 40960 | tf_op jit(solution)/shard_map/all_gather | solution.py:100
  335.9 1.9 fusion.6
  340.1 16.8 %reduce-scatter.9.cloned.1.call-done = f32[8,256]{1,0:T(8,128)} async-done(((f32[8,1024]{1,0:T(8,128)}), f32[8,256]{1,0:T(8,128)}) %reduce-scatter.9.cloned.1.call-update) | async-done | bytes 8208 | tf_op jit(solution)/shard_map/reduce_scatter | solution.py:113
  356.8 1.5 multiply_reduce_fusion.13
  358.3 43.2 %all-reduce = (f32[]{:T(128)}, f32[]{:T(128)}, f32[]{:T(128)}) all-reduce(f32[]{:T(128)} %get-tuple-element.15, f32[]{:T(128)} %get-tuple-element.14, f32[]{:T(128)} %get-tuple-element.13), channel_id=1, replica_groups=mesh['dom'=8,'dim'=4] {'dom','dim'}, use_global_device_ids=true, to_apply=%region_30.0 | all-reduce | flops 3 | bytes 24 | tf_op jit(solution)/shard_map/psum | solution.py:48
  405.4 11.4 %all_gather.54 = f32[8,1024]{1,0:T(8,128)S(1)} all-gather(f32[8,256]{1,0:T(8,128)S(1)} %multiply_add_fusion), channel_id=1, replica_groups=mesh['dom'=8,'dim'=4] {'dim'}, dimensions={1}, use_global_device_ids=true | all-gather | bytes 40960 | tf_op jit(solution)/shard_map/all_gather | solution.py:100
  417.1 2.0 fusion.7
  420.6 16.6 %reduce-scatter.11.cloned.1.call-done = f32[8,256]{1,0:T(8,128)} async-done(((f32[8,1024]{1,0:T(8,128)}), f32[8,256]{1,0:T(8,128)}) %reduce-scatter.11.cloned.1.call-update) | async-done | bytes 8208 | tf_op jit(solution)/shard_map/reduce_scatter | solution.py:113
  437.2 1.4 multiply_reduce_fusion.12
  438.6 43.1 %psum.149 = f32[]{:T(128)} all-reduce(f32[]{:T(128)} %multiply_reduce_fusion.12), channel_id=1, replica_groups=mesh['dom'=8,'dim'=4] {'dom','dim'}, use_global_device_ids=true, to_apply=%region_45.0 | all-reduce | flops 1 | bytes 8 | tf_op jit(solution)/shard_map/psum | solution.py:121
  (90 shorter events, 23.3 us)
Async XLA Ops:
  6.5 19.3 %all-to-all-start = ((bf16[8,16,256]{2,1,0:T(8,128)(2,1)}), bf16[8,16,256]{2,1,0:T(8,128)(2,1)S(1)}, u32[]{:S(2)}, u32[]{:S(2)}) async-start(bf16[8,16,256]{2,1,0:T(8,128)(2,1)} %param.4), calls=%async_computation | async-start | bytes 131072 | tf_op jit(solution)/shard_map/all_to_all | solution.py:64
  11.9 0.7 copy-start.2
  11.9 80.3 %all-reduce.9.cloned.1.call-start = ((), (), s32[]{:S(2)}) async-start(), calls=%async_computation.10 | async-start | bytes 198656 | tf_op jit(solution)/shard_map/psum | solution.py:87
  26.1 0.7 copy-start.5
  57.1 70.5 %reduce-scatter.5.cloned.1.call-start = ((), (), s32[]{:S(2)}) async-start(), calls=%async_computation.5 | async-start | bytes 40960 | tf_op jit(solution)/shard_map/reduce_scatter | solution.py:113
  92.1 0.6 copy-start.7
  105.8 0.8 copy-start.1
  110.1 97.9 %reduce-scatter.7.cloned.1.call-start = ((), (), s32[]{:S(2)}) async-start(), calls=%async_computation.6 | async-start | bytes 40960 | tf_op jit(solution)/shard_map/reduce_scatter | solution.py:113
  110.2 0.7 copy-start.4
  191.4 129.8 %all-reduce.7.cloned.1.call-start = ((), (), s32[]{:S(2)}) async-start(), calls=%async_computation.9 | async-start | bytes 198656 | tf_op jit(solution)/shard_map/psum | solution.py:87
  286.1 70.7 %reduce-scatter.9.cloned.1.call-start = ((), (), s32[]{:S(2)}) async-start(), calls=%async_computation.7 | async-start | bytes 40960 | tf_op jit(solution)/shard_map/reduce_scatter | solution.py:113
  321.2 0.6 copy-start.6
  335.0 0.8 copy-start
  339.3 97.9 %reduce-scatter.11.cloned.1.call-start = ((), (), s32[]{:S(2)}) async-start(), calls=%async_computation.8 | async-start | bytes 40960 | tf_op jit(solution)/shard_map/reduce_scatter | solution.py:113
  339.4 0.7 copy-start.3
Sparse Core Ops, SparseCore 0:
  57.3 34.8 all-reduce.8
  110.2 17.3 reduce-scatter.4
  191.5 16.4 reduce-scatter.6
  286.3 34.8 all-reduce.6
  339.4 17.3 reduce-scatter.8
  420.7 16.4 reduce-scatter.10
where the time goes:
time: 492 us; the launch traced here: 490 us
  blocking collectives  305 us (62%)
  waiting for transfers between devices  120 us (24%)
  between operations  22.8 us (5%)
  matrix products  21.7 us (4%)
  other arithmetic  9.23 us (2%)
  local copies, waits for them, and re-layouts  5.56 us (1%)
  starting transfers between devices  5.53 us (1%)
    psum x2, blocking collectives, residual_sum(): return lax.psum(jnp.sum(vectors * vectors), ('dom', 'dim'))  86.5 us
    psum x2, blocking collectives, per_device(): lax.psum((jnp.sum(direction * image), jnp.sum(residual * image), jnp.sum(...  86.1 us
    reduce_scatter x4, waiting for transfers between devices, per_device(): pairs = lax.psum_scatter(pairs, 'dim', scatter_dimension=1, tiled=True)  66.7 us
    psum x2, waiting for transfers between devices, per_device(): lax.psum((kernel_grad, kernel_pos, square_pos, kernel_total, square_total...  53 us
    all_gather x4, blocking collectives, per_device(): vectors_full = lax.all_gather(direction, 'dim', axis=1, tiled=True)  47.4 us
    all_gather x2, blocking collectives, per_device(): x_local = lax.all_gather(current, 'dim', axis=1, tiled=True)  24.5 us
    all_gather x2, blocking collectives, per_device(): lax.all_gather(own_pos, 'dom', axis=0, tiled=True)  17.5 us
    all_gather x2, blocking collectives, per_device(): lax.all_gather(own_grad, 'dom', axis=0, tiled=True)  17.5 us
  transfers between devices with their start and end apart: 7, of which 6 were waited for; matrix products, arithmetic and copies ran while one was open for 0% of the time, Pallas kernels for 0%

commit v1 on v0

--- a/solution.py
+++ b/solution.py
@@ -1,8 +1,10 @@
+import functools
 from functools import partial
 import jax
 import jax.numpy as jnp
 from jax import lax
 from jax.sharding import PartitionSpec as P
+from jax.lax import all_gather
 
 NEWTON = 2
 CG_STEPS = 2
@@ -11,6 +13,14 @@
 like_weight = 4.0
 move_size = 0.5
 highest = lax.Precision.HIGHEST
+
+
+def balance_runs_up(packet, which_axis, k_dim):
+    before = all_gather(packet, which_axis)
+    return jnp.concatenate(before, k_dim)
+
+
+try_all_unit = functools.partial(balance_runs_up, which_axis="dim", k_dim=1)
 
 
 def drift_terms(x_local, squares, kernel_scale, rows_pos, rows_grad):
@@ -97,7 +107,7 @@
         direction = drift
         norm_now = residual_sum(residual)
         for solve_step in range(CG_STEPS):
-            vectors_full = lax.all_gather(direction, "dim", axis=1, tiled=True)
+            vectors_full = try_all_unit(direction)
             start_total = jnp.zeros((part_rows, width), jnp.float32)
             block_step = partial(
                 pair_block,

time: 492 us -> 492 us (level)
  no operation moved by 1% of the time
where the time goes in v1:
time: 492 us; the launch traced here: 490 us
  blocking collectives  305 us (62%)
  waiting for transfers between devices  120 us (24%)
  between operations  22.8 us (5%)
  matrix products  21.7 us (4%)
  other arithmetic  9.23 us (2%)
  local copies, waits for them, and re-layouts  5.56 us (1%)
  starting transfers between devices  5.53 us (1%)
    psum x2, blocking collectives, residual_sum(): return lax.psum(jnp.sum(vectors * vectors), ('dom', 'dim'))  86.4 us
    psum x2, blocking collectives, per_device(): lax.psum((jnp.sum(direction * image), jnp.sum(residual * image), jnp.sum(...  86.1 us
    reduce_scatter x4, waiting for transfers between devices, per_device(): pairs = lax.psum_scatter(pairs, 'dim', scatter_dimension=1, tiled=True)  66.7 us
    psum x2, waiting for transfers between devices, per_device(): lax.psum((kernel_grad, kernel_pos, square_pos, kernel_total, square_total...  53 us
    all_gather x4, blocking collectives, balance_runs_up(): before = all_gather(packet, which_axis)  47.4 us
    all_gather x2, blocking collectives, per_device(): x_local = lax.all_gather(current, 'dim', axis=1, tiled=True)  24.5 us
    all_gather x2, blocking collectives, per_device(): lax.all_gather(own_pos, 'dom', axis=0, tiled=True)  17.5 us
    all_gather x2, blocking collectives, per_device(): lax.all_gather(own_grad, 'dom', axis=0, tiled=True)  17.5 us
  transfers between devices with their start and end apart: 7, of which 6 were waited for; matrix products, arithmetic and copies ran while one was open for 0% of the time, Pallas kernels for 0%

profile of v1, /device:TPU:12, one launch (start us, length us, event | category | flops | bytes accessed | tf_op | source)
XLA Modules:
  0.0 489.7 jit_solution(14536476329216031477)
XLA Ops:
  6.5 5.3 %all-to-all-start = ((bf16[8,16,256]{2,1,0:T(8,128)(2,1)}), bf16[8,16,256]{2,1,0:T(8,128)(2,1)S(1)}, u32[]{:S(2)}, u32[]{:S(2)}) async-start(bf16[8,16,256]{2,1,0:T(8,128)(2,1)} %param.4), calls=%async_computation | async-start | bytes 131072 | tf_op jit(solution)/shard_map/all_to_all | solution.py:74
  12.6 13.1 %all_gather.54 = f32[8,1024]{1,0:T(8,128)S(1)} all-gather(f32[8,256]{1,0:T(8,128)S(1)} %copy-done.2), channel_id=1, replica_groups=mesh['dom'=8,'dim'=4] {'dim'}, dimensions={1}, use_global_device_ids=true | all-gather | bytes 40960 | tf_op jit(solution)/shard_map/all_gather | solution.py:80
  27.0 9.2 %all-gather.4 = f32[8,2,1024]{2,1,0:T(2,128)S(1)} all-gather(f32[1,2,1024]{2,1,0:T(2,128)S(1)} %get-tuple-element.47), channel_id=1, replica_groups=mesh['dom'=8,'dim'=4] {'dom'}, dimensions={0}, use_global_device_ids=true | all-gather | bytes 73728 | tf_op jit(solution)/shard_map/all_gather | solution.py:89
  39.0 8.3 %all-gather.5 = f32[8,2,1024]{2,1,0:T(2,128)S(1)} all-gather(f32[1,2,1024]{2,1,0:T(2,128)S(1)} %get-tuple-element.48), channel_id=1, replica_groups=mesh['dom'=8,'dim'=4] {'dom'}, dimensions={0}, use_global_device_ids=true | all-gather | bytes 73728 | tf_op jit(solution)/shard_map/all_gather | solution.py:90
  48.2 8.9 %all-gather.6 = f32[8,2,16]{2,1,0:T(2,128)S(1)} all-gather(f32[1,2,16]{2,1,0:T(2,128)S(1)} %get-tuple-element.43), channel_id=1, replica_groups=mesh['dom'=8,'dim'=4] {'dom'}, dimensions={0}, use_global_device_ids=true | all-gather | bytes 1152 | tf_op jit(solution)/shard_map/all_gather | solution.py:91
  57.2 8.9 %all_gather.59 = bf16[16,16,1024]{2,1,0:T(8,128)(2,1)S(1)} all-gather(bf16[2,16,1024]{2,1,0:T(8,128)(2,1)S(1)} %all_to_all.16), channel_id=1, replica_groups=mesh['dom'=8,'dim'=4] {'dom'}, dimensions={0}, use_global_device_ids=true | all-gather | bytes 589824 | tf_op jit(solution)/shard_map/all_gather | solution.py:121
  66.1 26.1 %all-reduce.9.cloned.1.call-done = (f32[8,1024]{1,0:T(8,128)}, f32[8,1024]{1,0:T(8,128)}, f32[8]{0:T(128)}, f32[8,1024]{1,0:T(8,128)}, f32[8]{0:T(128)}) async-done(((f32[8,1024]{1,0:T(8,128)}, f32[8,1024]{1,0:T(8,128)}, f32[8]{0:T(128)}, f32[8,1024]{1,0:T(8,128)}, f32[8]{0:T(128)}), (f32[8,1024]{1,0:T(8,128)}, f32[8,1024]{1,0:T(8,128)}, f32[8]{0:T(128)}, f32[8,1024]{1,0:T(8,128)}, ...) | async-done | bytes 98384 | tf_op jit(solution)/shard_map/psum | solution.py:97
  93.6 12.2 %all-gather = f32[32,256]{1,0:T(8,128)S(1)} all-gather(f32[8,256]{1,0:T(8,128)S(1)} %fusion.14), channel_id=2, replica_groups=mesh['dom'=8,'dim'=4] {'dim'}, dimensions={0}, use_global_device_ids=true | all-gather | bytes 40960 | tf_op jit(solution)/shard_map/all_gather | solution.py:19
  106.7 1.9 fusion.4
  110.8 16.8 %reduce-scatter.5.cloned.1.call-done = f32[8,256]{1,0:T(8,128)} async-done(((f32[8,1024]{1,0:T(8,128)}), f32[8,256]{1,0:T(8,128)}) %reduce-scatter.5.cloned.1.call-update) | async-done | bytes 8208 | tf_op jit(solution)/shard_map/reduce_scatter | solution.py:123
  127.6 1.5 multiply_reduce_fusion.17
  129.1 43.2 %all-reduce.1 = (f32[]{:T(128)}, f32[]{:T(128)}, f32[]{:T(128)}) all-reduce(f32[]{:T(128)} %get-tuple-element.18, f32[]{:T(128)} %get-tuple-element.17, f32[]{:T(128)} %get-tuple-element.16), channel_id=1, replica_groups=mesh['dom'=8,'dim'=4] {'dom','dim'}, use_global_device_ids=true, to_apply=%region_7.0 | all-reduce | flops 3 | bytes 24 | tf_op jit(solution)/shard_map/psum | solution.py:58
  176.2 11.4 %all-gather.1 = f32[32,256]{1,0:T(8,128)S(1)} all-gather(f32[8,256]{1,0:T(8,128)S(1)} %multiply_add_fusion.3), channel_id=3, replica_groups=mesh['dom'=8,'dim'=4] {'dim'}, dimensions={0}, use_global_device_ids=true | all-gather | bytes 40960 | tf_op jit(solution)/shard_map/all_gather | solution.py:19
  187.9 2.0 fusion.5
  191.4 16.5 %reduce-scatter.7.cloned.1.call-done = f32[8,256]{1,0:T(8,128)} async-done(((f32[8,1024]{1,0:T(8,128)}), f32[8,256]{1,0:T(8,128)}) %reduce-scatter.7.cloned.1.call-update) | async-done | bytes 8208 | tf_op jit(solution)/shard_map/reduce_scatter | solution.py:123
  208.0 1.4 multiply_reduce_fusion.16
  209.3 43.1 %psum.140 = f32[]{:T(128)} all-reduce(f32[]{:T(128)} %multiply_reduce_fusion.16), channel_id=1, replica_groups=mesh['dom'=8,'dim'=4] {'dom','dim'}, use_global_device_ids=true, to_apply=%region_22.0 | all-reduce | flops 1 | bytes 8 | tf_op jit(solution)/shard_map/psum | solution.py:131
  253.1 11.4 %all_gather.63 = f32[8,1024]{1,0:T(8,128)S(1)} all-gather(f32[8,256]{1,0:T(8,128)S(1)} %get-tuple-element.50), channel_id=1, replica_groups=mesh['dom'=8,'dim'=4] {'dim'}, dimensions={1}, use_global_device_ids=true | all-gather | bytes 40960 | tf_op jit(solution)/shard_map/all_gather | solution.py:80
  265.0 8.3 %all-gather.7 = f32[8,2,1024]{2,1,0:T(2,128)S(1)} all-gather(f32[1,2,1024]{2,1,0:T(2,128)S(1)} %get-tuple-element.45), channel_id=1, replica_groups=mesh['dom'=8,'dim'=4] {'dom'}, dimensions={0}, use_global_device_ids=true | all-gather | bytes 73728 | tf_op jit(solution)/shard_map/all_gather | solution.py:89
  276.0 9.2 %all-gather.8 = f32[8,2,1024]{2,1,0:T(2,128)S(1)} all-gather(f32[1,2,1024]{2,1,0:T(2,128)S(1)} %get-tuple-element.46), channel_id=1, replica_groups=mesh['dom'=8,'dim'=4] {'dom'}, dimensions={0}, use_global_device_ids=true | all-gather | bytes 73728 | tf_op jit(solution)/shard_map/all_gather | solution.py:90
  286.3 8.0 %all-gather.9 = f32[8,2,16]{2,1,0:T(2,128)S(1)} all-gather(f32[1,2,16]{2,1,0:T(2,128)S(1)} %get-tuple-element.40), channel_id=1, replica_groups=mesh['dom'=8,'dim'=4] {'dom'}, dimensions={0}, use_global_device_ids=true | all-gather | bytes 1152 | tf_op jit(solution)/shard_map/all_gather | solution.py:91
  294.3 26.9 %all-reduce.7.cloned.1.call-done = (f32[8,1024]{1,0:T(8,128)}, f32[8,1024]{1,0:T(8,128)}, f32[8]{0:T(128)}, f32[8,1024]{1,0:T(8,128)}, f32[8]{0:T(128)}) async-done(((f32[8,1024]{1,0:T(8,128)}, f32[8,1024]{1,0:T(8,128)}, f32[8]{0:T(128)}, f32[8,1024]{1,0:T(8,128)}, f32[8]{0:T(128)}), (f32[8,1024]{1,0:T(8,128)}, f32[8,1024]{1,0:T(8,128)}, f32[8]{0:T(128)}, f32[8,1024]{1,0:T(8,128)}, ...) | async-done | bytes 98384 | tf_op jit(solution)/shard_map/psum | solution.py:97
  322.6 12.4 %all-gather.2 = f32[32,256]{1,0:T(8,128)S(1)} all-gather(f32[8,256]{1,0:T(8,128)S(1)} %fusion.12), channel_id=4, replica_groups=mesh['dom'=8,'dim'=4] {'dim'}, dimensions={0}, use_global_device_ids=true | all-gather | bytes 40960 | tf_op jit(solution)/shard_map/all_gather | solution.py:19
  335.9 1.9 fusion.6
  340.0 16.8 %reduce-scatter.9.cloned.1.call-done = f32[8,256]{1,0:T(8,128)} async-done(((f32[8,1024]{1,0:T(8,128)}), f32[8,256]{1,0:T(8,128)}) %reduce-scatter.9.cloned.1.call-update) | async-done | bytes 8208 | tf_op jit(solution)/shard_map/reduce_scatter | solution.py:123
  356.8 1.5 multiply_reduce_fusion.13
  358.3 43.2 %all-reduce = (f32[]{:T(128)}, f32[]{:T(128)}, f32[]{:T(128)}) all-reduce(f32[]{:T(128)} %get-tuple-element.15, f32[]{:T(128)} %get-tuple-element.14, f32[]{:T(128)} %get-tuple-element.13), channel_id=1, replica_groups=mesh['dom'=8,'dim'=4] {'dom','dim'}, use_global_device_ids=true, to_apply=%region_30.0 | all-reduce | flops 3 | bytes 24 | tf_op jit(solution)/shard_map/psum | solution.py:58
  405.4 11.4 %all-gather.3 = f32[32,256]{1,0:T(8,128)S(1)} all-gather(f32[8,256]{1,0:T(8,128)S(1)} %multiply_add_fusion), channel_id=5, replica_groups=mesh['dom'=8,'dim'=4] {'dim'}, dimensions={0}, use_global_device_ids=true | all-gather | bytes 40960 | tf_op jit(solution)/shard_map/all_gather | solution.py:19
  417.1 2.0 fusion.7
  420.6 16.6 %reduce-scatter.11.cloned.1.call-done = f32[8,256]{1,0:T(8,128)} async-done(((f32[8,1024]{1,0:T(8,128)}), f32[8,256]{1,0:T(8,128)}) %reduce-scatter.11.cloned.1.call-update) | async-done | bytes 8208 | tf_op jit(solution)/shard_map/reduce_scatter | solution.py:123
  437.1 1.4 multiply_reduce_fusion.12
  438.5 43.1 %psum.149 = f32[]{:T(128)} all-reduce(f32[]{:T(128)} %multiply_reduce_fusion.12), channel_id=1, replica_groups=mesh['dom'=8,'dim'=4] {'dom','dim'}, use_global_device_ids=true, to_apply=%region_45.0 | all-reduce | flops 1 | bytes 8 | tf_op jit(solution)/shard_map/psum | solution.py:131
  (90 shorter events, 23.3 us)
Async XLA Ops:
  6.5 19.3 %all-to-all-start = ((bf16[8,16,256]{2,1,0:T(8,128)(2,1)}), bf16[8,16,256]{2,1,0:T(8,128)(2,1)S(1)}, u32[]{:S(2)}, u32[]{:S(2)}) async-start(bf16[8,16,256]{2,1,0:T(8,128)(2,1)} %param.4), calls=%async_computation | async-start | bytes 131072 | tf_op jit(solution)/shard_map/all_to_all | solution.py:74
  11.9 0.7 copy-start.2
  11.9 80.3 %all-reduce.9.cloned.1.call-start = ((), (), s32[]{:S(2)}) async-start(), calls=%async_computation.10 | async-start | bytes 198656 | tf_op jit(solution)/shard_map/psum | solution.py:97
  26.1 0.7 copy-start.5
  57.1 70.5 %reduce-scatter.5.cloned.1.call-start = ((), (), s32[]{:S(2)}) async-start(), calls=%async_computation.5 | async-start | bytes 40960 | tf_op jit(solution)/shard_map/reduce_scatter | solution.py:123
  92.1 0.6 copy-start.7
  105.8 0.8 copy-start.1
  110.1 97.9 %reduce-scatter.7.cloned.1.call-start = ((), (), s32[]{:S(2)}) async-start(), calls=%async_computation.6 | async-start | bytes 40960 | tf_op jit(solution)/shard_map/reduce_scatter | solution.py:123
  110.2 0.7 copy-start.4
  191.4 129.8 %all-reduce.7.cloned.1.call-start = ((), (), s32[]{:S(2)}) async-start(), calls=%async_computation.9 | async-start | bytes 198656 | tf_op jit(solution)/shard_map/psum | solution.py:97
  286.1 70.7 %reduce-scatter.9.cloned.1.call-start = ((), (), s32[]{:S(2)}) async-start(), calls=%async_computation.7 | async-start | bytes 40960 | tf_op jit(solution)/shard_map/reduce_scatter | solution.py:123
  321.2 0.6 copy-start.6
  335.0 0.8 copy-start
  339.3 97.8 %reduce-scatter.11.cloned.1.call-start = ((), (), s32[]{:S(2)}) async-start(), calls=%async_computation.8 | async-start | bytes 40960 | tf_op jit(solution)/shard_map/reduce_scatter | solution.py:123
  339.3 0.7 copy-start.3
Sparse Core Ops, SparseCore 0:
  57.3 34.8 all-reduce.8
  110.2 17.3 reduce-scatter.4
  191.5 16.4 reduce-scatter.6
  286.2 34.8 all-reduce.6
  339.4 17.3 reduce-scatter.8
  420.7 16.4 reduce-scatter.10
